TPU v7x, 32 devices: a whole 2x2x4 slice. The times are simulated.
32 devices in a mesh: wide: 16 (over z, y, x), narrow: 2 (over core).
Axes of the slice: x: 2, y: 2, z: 4, core: 2. Of those that a mesh axis runs over, the one named last changes fastest.
Arguments:
- square_grads: bfloat16 [4, 8192, 8192], P(None, 'wide', 'narrow'), may hold values from -8.1 to 8.1
- narrow_grads: bfloat16 [4, 8192, 1024], P(None, 'wide', 'narrow'), may hold values from -8.1 to 8.1
- square_rowstate: float32 [4, 8192], P(None, 'wide'), may hold values from 0.0006 to 0.064
- square_colstate: float32 [4, 8192], P(None, 'narrow'), may hold values from 1e-05 to 2.1
- narrow_rowstate: float32 [4, 8192], P(None, 'wide'), may hold values from 0.0006 to 0.064
- narrow_colstate: float32 [4, 1024], P(None, 'narrow'), may hold values from 1e-05 to 2.1
Outputs:
- square_update: float32 [4, 8192, 8192], P(None, 'wide', 'narrow')
- narrow_update: float32 [4, 8192, 1024], P(None, 'wide', 'narrow')
- square_rowfactor: float32 [4, 8192], P(None, 'wide')
- square_colfactor: float32 [4, 8192], P(None, 'narrow')
- narrow_rowfactor: float32 [4, 8192], P(None, 'wide')
- narrow_colfactor: float32 [4, 1024], P(None, 'narrow')
All inputs are finite; a program needn't handle non-finite values.
Results may differ from a plain program's by a relative error of at most 0.0004.
Values sent between devices are 32-bit elements; how exact they have to be, the bound alone decides.
A program may use at most 128 MiB of HBM per device.

v0:
```python
import jax
import jax.numpy as jnp
from jax import lax
from jax.sharding import PartitionSpec as P

decay_rate = 0.9
epsilon_square = 1e-30
clip_limit = 1.0


def square_sums(grads):
    values = grads.astype(jnp.float32)
    squares = values * values + epsilon_square
    return (values, jnp.sum(squares, axis=2), jnp.sum(squares, axis=1))


def blend(state, total, count):
    return decay_rate * state + (1.0 - decay_rate) * (total / count)


def scaled(values, rowfactor, colfactor, row_mean):
    return (
        values
        * lax.rsqrt(rowfactor)[:, :, None]
        * lax.rsqrt(colfactor)[:, None, :]
        * jnp.sqrt(row_mean)[:, None, None]
    )


def clipped(raw, norm, entries):
    spread = jnp.sqrt(norm / entries)
    return raw / jnp.maximum(1.0, spread / clip_limit)[:, None, None]


def per_device(
    square_grads, narrow_grads, square_rowstate, square_colstate, narrow_rowstate, narrow_colstate
):
    total_rows = square_grads.shape[1] * lax.axis_size("wide")
    square_width = square_grads.shape[2] * lax.axis_size("narrow")
    narrow_width = narrow_grads.shape[2] * lax.axis_size("narrow")
    square_values, square_rowpart, square_colpart = square_sums(square_grads)
    narrow_values, narrow_rowpart, narrow_colpart = square_sums(narrow_grads)
    square_rowsum, narrow_rowsum = lax.psum((square_rowpart, narrow_rowpart), "narrow")
    square_colsum, narrow_colsum = lax.psum((square_colpart, narrow_colpart), "wide")
    square_rowfactor = blend(square_rowstate, square_rowsum, square_width)
    narrow_rowfactor = blend(narrow_rowstate, narrow_rowsum, narrow_width)
    square_colfactor = blend(square_colstate, square_colsum, total_rows)
    narrow_colfactor = blend(narrow_colstate, narrow_colsum, total_rows)
    square_rowtotal, narrow_rowtotal = lax.psum(
        (jnp.sum(square_rowfactor, axis=1), jnp.sum(narrow_rowfactor, axis=1)), "wide"
    )
    square_mean = square_rowtotal / total_rows
    narrow_mean = narrow_rowtotal / total_rows
    square_raw = scaled(square_values, square_rowfactor, square_colfactor, square_mean)
    narrow_raw = scaled(narrow_values, narrow_rowfactor, narrow_colfactor, narrow_mean)
    square_norm, narrow_norm = lax.psum(
        (
            jnp.sum(square_raw * square_raw, axis=(1, 2)),
            jnp.sum(narrow_raw * narrow_raw, axis=(1, 2)),
        ),
        ("wide", "narrow"),
    )
    square_update = clipped(square_raw, square_norm, total_rows * square_width)
    narrow_update = clipped(narrow_raw, narrow_norm, total_rows * narrow_width)
    return (
        square_update,
        narrow_update,
        square_rowfactor,
        square_colfactor,
        narrow_rowfactor,
        narrow_colfactor,
    )


def solution(mesh):
    placed = (
        P(None, "wide", "narrow"),
        P(None, "wide", "narrow"),
        P(None, "wide"),
        P(None, "narrow"),
        P(None, "wide"),
        P(None, "narrow"),
    )
    return jax.shard_map(
        per_device,
        mesh=mesh,
        in_specs=placed,
        out_specs=(
            P(None, "wide", "narrow"),
            P(None, "wide", "narrow"),
            P(None, "wide"),
            P(None, "narrow"),
            P(None, "wide"),
            P(None, "narrow"),
        ),
        check_vma=False,
    )
```

profile of v0, /device:TPU:0, one launch (start us, length us, event | category | flops | bytes accessed | tf_op | source)
XLA Modules:
  0.0 209.1 jit_solution(844003737577365710)
XLA Ops:
  7.2 0.0 copy-start
  7.2 0.0 copy-start.5
  7.2 0.0 copy-start.6
  7.2 0.0 copy-start.4
  7.2 0.0 copy-start.1
  7.2 0.0 all-reduce.5.cloned.1.call-start
  7.3 13.1 %fusion.1 = (f32[4,4096]{1,0:T(4,128)}, f32[4,512]{1,0:T(4,128)S(1)}) fusion(bf16[4,512,4096]{2,1,0:T(8,128)(2,1)} %param.6), kind=kLoop, calls=%fused_computation.3 | loop fusion | flops 41924608 | bytes 16850944 | tf_op jit(solution)/shard_map/reduce_sum | solution.py:14
  20.4 0.0 all-reduce.5.cloned.1.call-update
  20.4 0.0 copy-done
  20.4 1.0 fusion.9
  21.4 3.6 %all-reduce.2 = (f32[4,512]{1,0:T(4,128)S(1)}, f32[4,512]{1,0:T(4,128)S(1)}) all-reduce(f32[4,512]{1,0:T(4,128)S(1)} %get-tuple-element.7, f32[4,512]{1,0:T(4,128)S(1)} %get-tuple-element.9), channel_id=1, replica_groups=mesh['wide'=16,'narrow'=2] {'narrow'}, use_global_device_ids=true, to_apply=%region_1.0 | all-reduce | flops 4096 | bytes 32768 | tf_op jit(solution)/shard_map/psum | solution.py:43
  25.0 0.0 copy-done.5
  25.0 0.0 copy-done.6
  25.0 0.0 copy-start.2
  25.1 0.0 copy-start.3
  25.1 0.1 reduce_sum.74
  25.2 0.1 reduce_sum.78
  25.3 44.3 %all-reduce.1 = (f32[4]{0:T(128)S(1)}, f32[4]{0:T(128)S(1)}, f32[4,512]{1,0:T(4,128)S(1)}) all-reduce(f32[4]{0:T(128)S(1)} %reduce_sum.74, f32[4]{0:T(128)S(1)} %reduce_sum.78, f32[4,512]{1,0:T(4,128)S(1)} %get-tuple-element.8), channel_id=1, replica_groups=mesh['wide'=16,'narrow'=2] {'wide'}, use_global_device_ids=true, to_apply=%region_5.0 | all-reduce | flops 2056 | bytes 16448 | tf_op jit(solution)/shard_map/psum | solution.py:49
  69.6 0.0 copy-done.4
  69.7 0.6 fusion.17
  70.3 1.1 fusion.15
  71.4 55.4 %all-reduce.5.cloned.1.call-done = f32[4,4096]{1,0:T(4,128)} async-done(((f32[4,4096]{1,0:T(4,128)}), f32[4,4096]{1,0:T(4,128)}) %all-reduce.5.cloned.1.call-update) | async-done | bytes 65552 | tf_op jit(solution)/shard_map/psum | solution.py:44
  126.8 0.0 copy-done.1
  126.8 1.5 fusion.19
  128.3 12.6 %fusion.7 = f32[4]{0:T(128)S(1)} fusion(bf16[4,512,4096]{2,1,0:T(8,128)(2,1)} %param.6, f32[4]{0:T(128)S(1)} %multiply_sqrt_fusion.1, f32[4,4096]{1,0:T(4,128)S(1)} %get-tuple-element.23, f32[4,512]{1,0:T(4,128)S(1)} %get-tuple-element.25), kind=kLoop, calls=%fused_computation.9 | loop fusion | flops 50331644 | bytes 16850976 | tf_op jit(solution)/shard_map/reduce_sum | solution.py:58
  140.9 39.4 %all-reduce = (f32[4]{0:T(128)S(1)}, f32[4]{0:T(128)S(1)}) all-reduce(f32[4]{0:T(128)S(1)} %fusion.7, f32[4]{0:T(128)S(1)} %fusion.15), channel_id=1, replica_groups=mesh['wide'=16,'narrow'=2] {'wide','narrow'}, use_global_device_ids=true, to_apply=%region_7.0 | all-reduce | flops 8 | bytes 64 | tf_op jit(solution)/shard_map/psum | solution.py:56
  180.3 19.1 %fusion.5 = f32[4,512,4096]{2,1,0:T(8,128)} fusion(bf16[4,512,4096]{2,1,0:T(8,128)(2,1)} %param.6, f32[4]{0:T(128)S(1)} %sqrt_maximum_fusion.1, f32[4]{0:T(128)S(1)} %multiply_sqrt_fusion.1, f32[4,4096]{1,0:T(4,128)S(1)} %get-tuple-element.23, f32[4,512]{1,0:T(4,128)S(1)} %get-tuple-element.25), kind=kLoop, calls=%fused_computation.7 | loop fusion | flops 41943040 | bytes 50405408 | tf_op jit(solution)/shard_map/div | solution.py:32
  199.5 0.0 copy-done.2
  199.5 0.0 copy-done.3
  199.5 2.8 %fusion.13 = f32[4,512,512]{2,1,0:T(8,128)} fusion(bf16[4,512,512]{2,1,0:T(8,128)(2,1)S(1)} %copy-done, f32[4]{0:T(128)S(1)} %sqrt_maximum_fusion, f32[4]{0:T(128)S(1)} %multiply_sqrt_fusion, f32[4,512]{1,0:T(4,128)S(1)} %get-tuple-element.19, f32[4,512]{1,0:T(4,128)S(1)} %get-tuple-element.17), kind=kLoop, calls=%fused_computation.17 | loop fusion | flops 5242880 | bytes 6307872 | tf_op jit(solution)/shard_map/div | solution.py:32
  (5 shorter events, 0.0 us)
Async XLA Ops:
  7.2 13.2 %copy-start = (bf16[4,512,512]{2,1,0:T(8,128)(2,1)S(1)}, bf16[4,512,512]{2,1,0:T(8,128)(2,1)}, u32[]{:S(2)}) copy-start(bf16[4,512,512]{2,1,0:T(8,128)(2,1)} %param.7) | copy-start | bytes 6291460
  7.2 17.8 %copy-start.5 = (f32[4,512]{1,0:T(4,128)S(1)}, f32[4,512]{1,0:T(4,128)}, u32[]{:S(2)}) copy-start(f32[4,512]{1,0:T(4,128)} %param.10) | copy-start | bytes 24580
  7.2 17.8 %copy-start.6 = (f32[4,512]{1,0:T(4,128)S(1)}, f32[4,512]{1,0:T(4,128)}, u32[]{:S(2)}) copy-start(f32[4,512]{1,0:T(4,128)} %param.8) | copy-start | bytes 24580
  7.2 62.5 %copy-start.4 = (f32[4,512]{1,0:T(4,128)S(1)}, f32[4,512]{1,0:T(4,128)}, u32[]{:S(2)}) copy-start(f32[4,512]{1,0:T(4,128)} %param.11) | copy-start | bytes 24580
  7.2 119.6 %copy-start.1 = (f32[4,4096]{1,0:T(4,128)S(1)}, f32[4,4096]{1,0:T(4,128)}, u32[]{:S(2)}) copy-start(f32[4,4096]{1,0:T(4,128)} %param.9) | copy-start | bytes 196612
  7.2 119.6 %all-reduce.5.cloned.1.call-start = ((), (), s32[]{:S(2)}) async-start(), calls=%async_computation | async-start | bytes 131072 | tf_op jit(solution)/shard_map/psum | solution.py:44
  25.0 174.4 %copy-start.2 = (f32[4,512]{1,0:T(4,128)}, f32[4,512]{1,0:T(4,128)S(1)}, u32[]{:S(2)}) copy-start(f32[4,512]{1,0:T(4,128)S(1)} %get-tuple-element.18) | copy-start | bytes 24580
  25.1 174.4 %copy-start.3 = (f32[4,512]{1,0:T(4,128)}, f32[4,512]{1,0:T(4,128)S(1)}, u32[]{:S(2)}) copy-start(f32[4,512]{1,0:T(4,128)S(1)} %get-tuple-element.26) | copy-start | bytes 24580
Sparse Core Ops, SparseCore 0:
  20.5 106.1 all-reduce.4
where the time goes:
time: 210 us; the launch traced here: 209 us
  blocking collectives  87.4 us (42%)
  waiting for transfers between devices  55.4 us (26%)
  other arithmetic  52.1 us (25%)
  between operations  14.1 us (7%)
    psum x1, waiting for transfers between devices, per_device(): lax.psum((square_colpart, narrow_colpart), 'wide')  55.4 us
    psum x1, blocking collectives, per_device(): lax.psum((jnp.sum(square_rowfactor, axis=1), jnp.sum(narrow_rowfactor, ax...  44.3 us
    psum x1, blocking collectives, per_device(): lax.psum((jnp.sum(square_raw * square_raw, axis=(1, 2)), jnp.sum(narrow_r...  39.4 us
    div x2, other arithmetic, clipped(): return raw / jnp.maximum(1.0, spread / clip_limit)[:, None, None]  21.9 us
    reduce_sum x2, other arithmetic, square_sums(): return (values, jnp.sum(squares, axis=2), jnp.sum(squares, axis=1))  14.1 us
    reduce_sum x1, other arithmetic, per_device(): jnp.sum(square_raw * square_raw, axis=(1, 2))  12.6 us
  transfers between devices with their start and end apart: 1, of which 1 were waited for; matrix products, arithmetic and copies ran while one was open for 1% of the time, Pallas kernels for 0%

commit v1 on v0

--- a/solution.py
+++ b/solution.py
@@ -1,11 +1,17 @@
+import functools
+
 import jax
 import jax.numpy as jnp
 from jax import lax
+from jax.experimental import pallas as pl
+from jax.experimental.pallas import tpu as pltpu
 from jax.sharding import PartitionSpec as P
 
 decay_rate = 0.9
 epsilon_square = 1e-30
 clip_limit = 1.0
+LANES = 128
+AHEAD = 6
 
 
 def square_sums(grads):
@@ -32,7 +38,7 @@
     return raw / jnp.maximum(1.0, spread / clip_limit)[:, None, None]
 
 
-def per_device(
+def plain_per_device(
     square_grads, narrow_grads, square_rowstate, square_colstate, narrow_rowstate, narrow_colstate
 ):
     total_rows = square_grads.shape[1] * lax.axis_size("wide")
@@ -72,7 +78,412 @@
     )
 
 
+def tiled(x, count):
+    return jnp.concatenate([x] * count, axis=1) if count > 1 else x
+
+
+def fold(values):
+    out = values[0:8]
+    for i in range(8, values.shape[0], 8):
+        out = out + values[i : i + 8]
+    return out
+
+
+def picked_row(values, index):
+    row = lax.broadcasted_iota(jnp.int32, values.shape, 0)
+    return jnp.sum(jnp.where(row == index, values, 0.0), axis=0, keepdims=True)
+
+
+def column_block(cols):
+    block = 1024
+    while cols % block:
+        block //= 2
+    return block
+
+
+def stats_kernel(
+    wide, narrow,
+    sq_hbm, na_hbm, sq_rs, sq_cs, na_rs, na_cs,
+    sq_rf, sq_cf, na_rf, na_cf, scale_out,
+    sq_buf, na_buf, rowpart, rowinv, row_mine, row_theirs, col_mine, col_theirs, col_all,
+    sq_w, na_w, table, finals,
+    in_sems, row_send, row_recv, rs_send, rs_recv, ag_send, ag_recv, fin_send, fin_recv,
+):
+    count, rows, sq_cols = sq_hbm.shape
+    na_cols = na_hbm.shape[2]
+    total_rows = rows * wide
+    me_w, me_n = lax.axis_index("wide"), lax.axis_index("narrow")
+    me = me_w * narrow + me_n
+    devices = wide * narrow
+    step = 16
+    mesh_id = pl.DeviceIdType.MESH
+
+    def device(index):
+        return (index // narrow, lax.rem(index, narrow))
+
+    mats = []
+    for m in range(count):
+        mats.append((sq_hbm, sq_buf, sq_w, sq_rs, sq_rf, sq_cols, m, m))
+        mats.append((na_hbm, na_buf, na_w, na_rs, na_rf, na_cols, m, count + m))
+
+    chunks = []
+    for hbm, buf, _, _, _, cols, m, _ in mats:
+        block = column_block(cols)
+        for start in range(0, cols, block):
+            chunks.append((hbm, buf, m, start, block))
+    copies = [
+        pltpu.make_async_copy(
+            hbm.at[m, :, pl.ds(start, block)], buf.at[m, :, pl.ds(start, block)], in_sems.at[i]
+        )
+        for i, (hbm, buf, m, start, block) in enumerate(chunks)
+    ]
+    for copy in copies[:AHEAD]:
+        copy.start()
+
+    barrier = pltpu.get_barrier_semaphore()
+
+    @pl.loop(1, devices)
+    def _(d):
+        pl.semaphore_signal(
+            barrier, inc=1, device_id=device(lax.rem(me + d, devices)), device_id_type=mesh_id
+        )
+
+    sq_per = sq_cols // LANES // wide
+    na_blocks = na_cols // LANES
+    na_per = count * na_blocks // wide
+
+    def home(cols, m, block):
+        if cols == sq_cols:
+            return block // sq_per, m * sq_per + block % sq_per
+        index = m * na_blocks + block
+        return index // na_per, count * sq_per + index % na_per
+
+    def row_copy(i):
+        return pltpu.make_async_remote_copy(
+            src_ref=row_mine.at[i],
+            dst_ref=row_theirs.at[i],
+            send_sem=row_send.at[i],
+            recv_sem=row_recv.at[i],
+            device_id=(me_w, 1 - me_n),
+            device_id_type=mesh_id,
+        )
+
+    done = 0
+    for order, (_, buf, _, _, _, cols, m, i) in enumerate(mats):
+        block = column_block(cols)
+        for start in range(0, cols, block):
+            copies[done].wait()
+            if done + AHEAD < len(copies):
+                copies[done + AHEAD].start()
+            done += 1
+
+            def body(r, acc, buf=buf, m=m, start=start, block=block):
+                at = pl.ds(pl.multiple_of(r * step, step), step)
+                values = buf[m, at, pl.ds(start, block)].astype(jnp.float32)
+                squares = values * values
+                part = squares[:, 0:LANES]
+                for k in range(LANES, block, LANES):
+                    part = part + squares[:, k : k + LANES]
+                if start:
+                    part = part + rowpart[at, :]
+                rowpart[at, :] = part
+                return acc + fold(squares)
+
+            acc = lax.fori_loop(
+                0, rows // step, body, jnp.zeros((8, block), jnp.float32), unroll=2
+            )
+            sums = jnp.sum(acc, axis=0, keepdims=True)
+            for b in range(block // LANES):
+                owner, row = home(cols, m, start // LANES + b)
+                col_mine[owner, row : row + 1, :] = sums[:, b * LANES : (b + 1) * LANES]
+        for q in range(rows // LANES):
+            square = rowpart[q * LANES : (q + 1) * LANES, :].T
+            row_mine[i, q : q + 1, :] = jnp.sum(square, axis=0, keepdims=True)
+        if order == 0:
+            pl.semaphore_wait(barrier, devices - 1)
+        row_copy(i).start()
+
+    def rs_copy(d):
+        peer = lax.rem(me_w + d, wide)
+        return pltpu.make_async_remote_copy(
+            src_ref=col_mine.at[peer],
+            dst_ref=col_theirs.at[d],
+            send_sem=rs_send.at[d],
+            recv_sem=rs_recv.at[d],
+            device_id=(peer, me_n),
+            device_id_type=mesh_id,
+        )
+
+    @pl.loop(1, wide)
+    def _(d):
+        rs_copy(d).start()
+
+    def ag_copy(d):
+        peer = lax.rem(me_w + d, wide)
+        return pltpu.make_async_remote_copy(
+            src_ref=col_all.at[me_w],
+            dst_ref=col_all.at[me_w],
+            send_sem=ag_send.at[d],
+            recv_sem=ag_recv.at[me_w],
+            device_id=(peer, me_n),
+            device_id_type=mesh_id,
+        )
+
+    def own_columns():
+        @pl.loop(1, wide)
+        def _(d):
+            rs_copy(d).wait_recv()
+
+        total = col_mine[me_w]
+        for d in range(1, wide):
+            total = total + col_theirs[d]
+
+        def put(row, state):
+            mean = total[row : row + 1] / total_rows + epsilon_square
+            col_all[me_w, row : row + 1, :] = decay_rate * state + (1.0 - decay_rate) * mean
+
+        for m in range(count):
+            for b in range(sq_per):
+                at = pl.multiple_of((me_w * sq_per + b) * LANES, LANES)
+                put(m * sq_per + b, sq_cs[m : m + 1, pl.ds(at, LANES)])
+        for b in range(na_per):
+            index = me_w * na_per + b
+            at = pl.multiple_of(lax.rem(index, na_blocks) * LANES, LANES)
+            put(count * sq_per + b, picked_row(na_cs[:, pl.ds(at, LANES)], index // na_blocks))
+
+        @pl.loop(1, wide)
+        def _(d):
+            ag_copy(d).start()
+
+    for order, (_, buf, w, rs, rf, cols, m, i) in enumerate(mats):
+        if order == 5:
+            own_columns()
+        row_copy(i).wait_recv()
+        width = cols * narrow
+        factors = jnp.zeros((1, LANES), jnp.float32)
+        for q in range(rows // LANES):
+            lanes = slice(q * LANES, (q + 1) * LANES)
+            mean = (row_mine[i, q : q + 1, :] + row_theirs[i, q : q + 1, :]) / width
+            factor = decay_rate * rs[m : m + 1, lanes] + (1.0 - decay_rate) * (
+                mean + epsilon_square
+            )
+            rf[m : m + 1, lanes] = factor
+            factors = factors + factor
+            root = lax.rsqrt(factor)
+            rowinv[lanes, :] = jnp.broadcast_to(root * root, (LANES, LANES)).T
+        table[2 * count + i : 2 * count + i + 1, :] = factors
+        block = column_block(cols)
+        for start in range(0, cols, block):
+
+            def body(r, acc, buf=buf, m=m, start=start, block=block):
+                at = pl.ds(pl.multiple_of(r * step, step), step)
+                values = buf[m, at, pl.ds(start, block)].astype(jnp.float32)
+                inv = tiled(rowinv[at, :], block // LANES)
+                return acc + fold(values * values * inv)
+
+            w[m, :, start : start + block] = lax.fori_loop(
+                0, rows // step, body, jnp.zeros((8, block), jnp.float32), unroll=2
+            )
+
+    @pl.loop(1, wide)
+    def _(d):
+        source = lax.rem(me_w + d, wide)
+        pltpu.make_async_remote_copy(
+            src_ref=col_all.at[source],
+            dst_ref=col_all.at[source],
+            send_sem=ag_send.at[d],
+            recv_sem=ag_recv.at[source],
+            device_id=(source, me_n),
+            device_id_type=mesh_id,
+        ).wait_recv()
+
+    for _, _, w, _, _, cols, m, i in mats:
+        cf = sq_cf if cols == sq_cols else na_cf
+        part = jnp.zeros((8, LANES), jnp.float32)
+        for b in range(cols // LANES):
+            owner, row = home(cols, m, b)
+            lanes = slice(b * LANES, (b + 1) * LANES)
+            factor = col_all[owner, row : row + 1, :]
+            cf[m : m + 1, lanes] = factor
+            root = lax.rsqrt(factor)
+            part = part + w[m, :, lanes] * (root * root)
+        table[i : i + 1, :] = jnp.sum(part, axis=0, keepdims=True)
+
+    height = 4 * count
+    lane = lax.broadcasted_iota(jnp.int32, (height, LANES), 1)
+    sub = lax.broadcasted_iota(jnp.int32, (height, LANES), 0)
+    sums = jnp.sum(table[...], axis=1, keepdims=True)
+    finals[me] = jnp.sum(jnp.where(lane == sub, sums, 0.0), axis=0, keepdims=True)
+
+    def fin_copy(slot, d, peer):
+        return pltpu.make_async_remote_copy(
+            src_ref=finals.at[slot],
+            dst_ref=finals.at[slot],
+            send_sem=fin_send.at[d],
+            recv_sem=fin_recv.at[slot],
+            device_id=device(peer),
+            device_id_type=mesh_id,
+        )
+
+    @pl.loop(1, devices)
+    def _(d):
+        fin_copy(me, d, lax.rem(me + d, devices)).start()
+
+    for i in range(2 * count):
+        row_copy(i).wait_send()
+
+    @pl.loop(1, wide)
+    def _(d):
+        rs_copy(d).wait_send()
+        ag_copy(d).wait_send()
+
+    @pl.loop(1, devices)
+    def _(d):
+        source = lax.rem(me + d, devices)
+        fin_copy(source, d, source).wait_recv()
+
+    total = finals[0]
+    for k in range(1, devices):
+        total = total + finals[k]
+    mean = pltpu.roll(total, LANES - 2 * count, axis=1) / (total_rows * narrow)
+    place = lax.broadcasted_iota(jnp.int32, (1, LANES), 1)
+    entries = jnp.where(
+        place < count, float(total_rows * sq_cols * narrow), float(total_rows * na_cols * narrow)
+    )
+    spread = jnp.sqrt(mean * total / entries)
+    scale = jnp.sqrt(mean) / jnp.maximum(1.0, spread / clip_limit)
+    lane = lax.broadcasted_iota(jnp.int32, (2 * count, LANES), 1)
+    sub = lax.broadcasted_iota(jnp.int32, (2 * count, LANES), 0)
+    picked = jnp.sum(jnp.where(lane == sub, scale, 0.0), axis=1, keepdims=True)
+    scale_out[...] = jnp.broadcast_to(picked, (2 * count, LANES))
+
+    @pl.loop(1, devices)
+    def _(d):
+        fin_copy(me, d, lax.rem(me + d, devices)).wait_send()
+
+
+def update_kernel(
+    count,
+    sq_g, na_g, sq_rf, sq_cf, na_rf, na_cf, scale,
+    sq_out, na_out, sq_rf_out, sq_cf_out, na_rf_out, na_cf_out,
+):
+    m, q = pl.program_id(0), pl.program_id(1)
+    at = pl.multiple_of(q * LANES, LANES)
+
+    @pl.when((m == 0) & (q == 0))
+    def _():
+        sq_rf_out[...] = sq_rf[...]
+        sq_cf_out[...] = sq_cf[...]
+        na_rf_out[...] = na_rf[...]
+        na_cf_out[...] = na_cf[...]
+
+    for g, rf, cf, out, first in (
+        (sq_g, sq_rf, sq_cf, sq_out, 0),
+        (na_g, na_rf, na_cf, na_out, count),
+    ):
+        rowmul = lax.rsqrt(picked_row(rf[:, pl.ds(at, LANES)], m)) * scale[pl.ds(first + m, 1), :]
+        rowmul = jnp.broadcast_to(rowmul, (LANES, LANES)).T
+        cols = g.shape[2]
+        block = min(cols, 512)
+        for start in range(0, cols, block):
+            colmul = lax.rsqrt(cf[pl.ds(m, 1), pl.ds(start, block)])
+            values = g[0, :, pl.ds(start, block)].astype(jnp.float32)
+            out[0, :, pl.ds(start, block)] = values * tiled(rowmul, block // LANES) * colmul
+
+
+def kernel_per_device(wide, narrow, square_grads, narrow_grads, *states):
+    count, rows, sq_cols = square_grads.shape
+    na_cols = narrow_grads.shape[2]
+    f32 = jnp.float32
+    vmem = pl.BlockSpec(memory_space=pltpu.VMEM)
+    hbm = pl.BlockSpec(memory_space=pl.ANY)
+    shape = jax.ShapeDtypeStruct
+    table_rows = count * (sq_cols + na_cols) // LANES // wide
+    chunks = count * (sq_cols // column_block(sq_cols) + na_cols // column_block(na_cols))
+    dma = pltpu.SemaphoreType.DMA
+    factors = (
+        shape((count, rows), f32),
+        shape((count, sq_cols), f32),
+        shape((count, rows), f32),
+        shape((count, na_cols), f32),
+    )
+    stats = pl.pallas_call(
+        functools.partial(stats_kernel, wide, narrow),
+        out_shape=factors + (shape((2 * count, LANES), f32),),
+        in_specs=[hbm, hbm, vmem, vmem, vmem, vmem],
+        out_specs=[vmem] * 5,
+        scratch_shapes=[
+            pltpu.VMEM((count, rows, sq_cols), square_grads.dtype),
+            pltpu.VMEM((count, rows, na_cols), narrow_grads.dtype),
+            pltpu.VMEM((rows, LANES), f32),
+            pltpu.VMEM((rows, LANES), f32),
+            pltpu.VMEM((2 * count, rows // LANES, LANES), f32),
+            pltpu.VMEM((2 * count, rows // LANES, LANES), f32),
+            pltpu.VMEM((wide, table_rows, LANES), f32),
+            pltpu.VMEM((wide, table_rows, LANES), f32),
+            pltpu.VMEM((wide, table_rows, LANES), f32),
+            pltpu.VMEM((count, 8, sq_cols), f32),
+            pltpu.VMEM((count, 8, na_cols), f32),
+            pltpu.VMEM((4 * count, LANES), f32),
+            pltpu.VMEM((wide * narrow, 1, LANES), f32),
+            dma((chunks,)),
+            dma((2 * count,)),
+            dma((2 * count,)),
+            dma((wide,)),
+            dma((wide,)),
+            dma((wide,)),
+            dma((wide,)),
+            dma((wide * narrow,)),
+            dma((wide * narrow,)),
+        ],
+        compiler_params=pltpu.CompilerParams(
+            collective_id=0, has_side_effects=True, vmem_limit_bytes=40 * 2**20
+        ),
+        name="stats",
+    )(square_grads, narrow_grads, *states)
+
+    full = lambda s: pl.BlockSpec(s.shape, lambda m, q: (0, 0))
+    blocked = lambda cols: pl.BlockSpec((1, LANES, cols), lambda m, q: (m, q, 0))
+    square_update, narrow_update, *small = pl.pallas_call(
+        functools.partial(update_kernel, count),
+        grid=(count, rows // LANES),
+        out_shape=(
+            shape(square_grads.shape, f32),
+            shape(narrow_grads.shape, f32),
+        )
+        + factors,
+        in_specs=[blocked(sq_cols), blocked(na_cols)]
+        + [full(s) for s in factors]
+        + [pl.BlockSpec((2 * count, LANES), lambda m, q: (0, 0))],
+        out_specs=[blocked(sq_cols), blocked(na_cols)] + [full(s) for s in factors],
+        compiler_params=pltpu.CompilerParams(
+            dimension_semantics=("arbitrary", "arbitrary"), vmem_limit_bytes=20 * 2**20
+        ),
+        name="update",
+    )(square_grads, narrow_grads, *stats)
+    return (square_update, narrow_update, *small)
+
+
 def solution(mesh):
+    wide, narrow = mesh.shape["wide"], mesh.shape["narrow"]
+
+    def per_device(square_grads, narrow_grads, *states):
+        count, rows, sq_cols = square_grads.shape
+        na_cols = narrow_grads.shape[2]
+        whole_tiles = (
+            narrow == 2
+            and wide > 1
+            and rows % LANES == 0
+            and sq_cols % (LANES * wide) == 0
+            and na_cols % LANES == 0
+            and sq_cols != na_cols
+            and (count * na_cols) % (LANES * wide) == 0
+            and 4 * count <= LANES
+        )
+        if whole_tiles:
+            return kernel_per_device(wide, narrow, square_grads, narrow_grads, *states)
+        return plain_per_device(square_grads, narrow_grads, *states)
+
     placed = (
         P(None, "wide", "narrow"),
         P(None, "wide", "narrow"),
@@ -85,13 +496,6 @@
         per_device,
         mesh=mesh,
         in_specs=placed,
-        out_specs=(
-            P(None, "wide", "narrow"),
-            P(None, "wide", "narrow"),
-            P(None, "wide"),
-            P(None, "narrow"),
-            P(None, "wide"),
-            P(None, "narrow"),
-        ),
+        out_specs=placed,
         check_vma=False,
     )

time: 210 us -> 52.3 us (0.25)
  blocking collectives: 87.4 us -> 0 us
  waiting for transfers between devices: 55.4 us -> 0 us
  other arithmetic: 52.1 us -> 0 us
  Pallas kernels: 0 us -> 45.5 us
  between operations: 14.1 us -> 0.67 us
  local copies, waits for them, and re-layouts: 0.03 us -> 5.8 us
    psum x3 -> x0, blocking collectives: 87.4 us -> none  [the longest x1 44.3 us: per_device(): lax.psum((jnp.sum(square_rowfactor, axis=1), jnp.sum(narrow_rowfactor, ax...]
    psum x1 -> x0, waiting for transfers between devices: 55.4 us -> none  [per_device(): lax.psum((square_colpart, narrow_colpart), 'wide')]
    pallas_call x0 -> x2, Pallas kernels: none -> 45.5 us  [the longest x1 30.6 us: kernel_per_device(): pl.pallas_call(functools.partial(stats_kernel, wide, narrow), out_shape=f...]
    reduce_sum x6 -> x0, other arithmetic: 28.1 us -> none  [the longest x2 14.1 us: square_sums(): return (values, jnp.sum(squares, axis=2), jnp.sum(squares, axis=1))]
    div x2 -> x0, other arithmetic: 21.9 us -> none  [clipped(): return raw / jnp.maximum(1.0, spread / clip_limit)[:, None, None]]
    unnamed x14 -> x12, local copies, waits for them, and re-layouts: 0.03 us -> 5.8 us
    rsqrt x3 -> x0, other arithmetic: 2.12 us -> none  [the longest x2 2.11 us: scaled(): lax.rsqrt(colfactor)[:, None, :]]
  transfers between devices with their start and end apart: 1 -> 0, of which waited for: 1 -> 0; matrix products, arithmetic and copies ran while one was open for 1% -> 0% of each run, Pallas kernels for 0% -> 0%
where the time goes in v1:
time: 52.3 us; the launch traced here: 52 us
  Pallas kernels  45.5 us (87%)
  local copies, waits for them, and re-layouts  5.8 us (11%)
  between operations  0.67 us (1%)
    pallas_call x1, Pallas kernels, kernel_per_device(): pl.pallas_call(functools.partial(stats_kernel, wide, narrow), out_shape=f...  30.6 us
    pallas_call x1, Pallas kernels, kernel_per_device(): pl.pallas_call(functools.partial(update_kernel, count), grid=(count, rows...  15 us
    unnamed x12, local copies, waits for them, and re-layouts  5.8 us

profile of v1, /device:TPU:0, one launch (start us, length us, event | category | flops | bytes accessed | tf_op | source)
XLA Modules:
  0.0 52.0 jit_solution(11393814455927763606)
XLA Ops:
  0.6 0.0 copy-start
  0.6 0.0 copy-start.1
  0.7 1.7 %copy-done.1 = bf16[4,512,512]{2,1,0:T(8,128)(2,1)S(1)} copy-done((bf16[4,512,512]{2,1,0:T(8,128)(2,1)S(1)}, bf16[4,512,512]{2,1,0:T(8,128)(2,1)}, u32[]{:S(2)}) %copy-start.1) | copy-done | bytes 2097176
  2.4 0.0 copy-start.2
  2.4 1.1 %copy-done.2 = f32[4,4096]{1,0:T(4,128)S(1)} copy-done((f32[4,4096]{1,0:T(4,128)S(1)}, f32[4,4096]{1,0:T(4,128)}, u32[]{:S(2)}) %copy-start.2) | copy-done | bytes 65560
  3.5 0.0 copy-start.3
  3.5 1.0 %copy-done.3 = f32[4,512]{1,0:T(4,128)S(1)} copy-done((f32[4,512]{1,0:T(4,128)S(1)}, f32[4,512]{1,0:T(4,128)}, u32[]{:S(2)}) %copy-start.3) | copy-done | bytes 8216
  4.5 0.0 copy-start.4
  4.5 1.0 %copy-done.4 = f32[4,512]{1,0:T(4,128)S(1)} copy-done((f32[4,512]{1,0:T(4,128)S(1)}, f32[4,512]{1,0:T(4,128)}, u32[]{:S(2)}) %copy-start.4) | copy-done | bytes 8216
  5.5 0.0 copy-start.5
  5.5 1.0 %copy-done.5 = f32[4,512]{1,0:T(4,128)S(1)} copy-done((f32[4,512]{1,0:T(4,128)S(1)}, f32[4,512]{1,0:T(4,128)}, u32[]{:S(2)}) %copy-start.5) | copy-done | bytes 8216
  6.4 30.6 %stats.1 = (f32[4,512]{1,0:T(4,128)S(1)}, f32[4,4096]{1,0:T(4,128)S(1)}, f32[4,512]{1,0:T(4,128)S(1)}, f32[4,512]{1,0:T(4,128)S(1)}, f32[8,128]{1,0:T(8,128)S(1)}) custom-call(bf16[4,512,4096]{2,1,0:T(8,128)(2,1)} %sq_g.1, bf16[4,512,512]{2,1,0:T(8,128)(2,1)S(1)} %copy-done.1, f32[4,512]{1,0:T(4,128)S(1)} %copy-done.3, f32[4,4096]{1,0:T(4,128)S(1)} %copy-done.2, ...), custom_call_target="tpu_custom_call" | custom-call | tf_op jit(solution)/shard_map/stats/pallas_call | solution.py:410
  37.0 0.0 copy-done
  37.0 15.0 %update.1 = (f32[4,512,4096]{2,1,0:T(8,128)}, f32[4,512,512]{2,1,0:T(8,128)}, f32[4,512]{1,0:T(4,128)}, f32[4,4096]{1,0:T(4,128)}, f32[4,512]{1,0:T(4,128)}, /*index=5*/f32[4,512]{1,0:T(4,128)}) custom-call(bf16[4,512,4096]{2,1,0:T(8,128)(2,1)S(1)} %copy-done, bf16[4,512,512]{2,1,0:T(8,128)(2,1)S(1)} %copy-done.1, f32[4,512]{1,0:T(4,128)S(1)} %get-tuple-element.11.sq_rf, ...), custom_call_target="tpu_custom_call" | custom-call | tf_op jit(solution)/shard_map/update/pallas_call | solution.py:447
Async XLA Ops:
  0.6 36.4 %copy-start = (bf16[4,512,4096]{2,1,0:T(8,128)(2,1)S(1)}, bf16[4,512,4096]{2,1,0:T(8,128)(2,1)}, u32[]{:S(2)}) copy-start(bf16[4,512,4096]{2,1,0:T(8,128)(2,1)} %sq_g.1) | copy-start | bytes 50331652
  0.6 1.7 %copy-start.1 = (bf16[4,512,512]{2,1,0:T(8,128)(2,1)S(1)}, bf16[4,512,512]{2,1,0:T(8,128)(2,1)}, u32[]{:S(2)}) copy-start(bf16[4,512,512]{2,1,0:T(8,128)(2,1)} %na_g.1) | copy-start | bytes 6291460
  2.4 1.1 %copy-start.2 = (f32[4,4096]{1,0:T(4,128)S(1)}, f32[4,4096]{1,0:T(4,128)}, u32[]{:S(2)}) copy-start(f32[4,4096]{1,0:T(4,128)} %sq_cs.1) | copy-start | bytes 196612
  3.5 1.0 %copy-start.3 = (f32[4,512]{1,0:T(4,128)S(1)}, f32[4,512]{1,0:T(4,128)}, u32[]{:S(2)}) copy-start(f32[4,512]{1,0:T(4,128)} %sq_rs.1) | copy-start | bytes 24580
  4.5 1.0 %copy-start.4 = (f32[4,512]{1,0:T(4,128)S(1)}, f32[4,512]{1,0:T(4,128)}, u32[]{:S(2)}) copy-start(f32[4,512]{1,0:T(4,128)} %na_rs.1) | copy-start | bytes 24580
  5.5 1.0 %copy-start.5 = (f32[4,512]{1,0:T(4,128)S(1)}, f32[4,512]{1,0:T(4,128)}, u32[]{:S(2)}) copy-start(f32[4,512]{1,0:T(4,128)} %na_cs.1) | copy-start | bytes 24580

commit v2 on v1

--- a/solution.py
+++ b/solution.py
@@ -103,11 +103,11 @@
 
 def stats_kernel(
     wide, narrow,
-    sq_hbm, na_hbm, sq_rs, sq_cs, na_rs, na_cs,
-    sq_rf, sq_cf, na_rf, na_cf, scale_out,
-    sq_buf, na_buf, rowpart, rowinv, row_mine, row_theirs, col_mine, col_theirs, col_all,
+    sq_hbm, na_hbm, sq_rs_hbm, sq_cs_hbm, na_rs_hbm, na_cs_hbm,
+    sq_rf, sq_cf, na_rf, na_cf, scale_out, sq_buf, na_buf,
+    sq_rs, sq_cs, na_rs, na_cs, rowpart, rowinv, row_mine, row_theirs, col_mine, col_theirs, col_all,
     sq_w, na_w, table, finals,
-    in_sems, row_send, row_recv, rs_send, rs_recv, ag_send, ag_recv, fin_send, fin_recv,
+    in_sems, state_sems, row_send, row_recv, rs_send, rs_recv, ag_send, ag_recv, fin_send, fin_recv,
 ):
     count, rows, sq_cols = sq_hbm.shape
     na_cols = na_hbm.shape[2]
@@ -137,7 +137,13 @@
         )
         for i, (hbm, buf, m, start, block) in enumerate(chunks)
     ]
-    for copy in copies[:AHEAD]:
+    states = [
+        pltpu.make_async_copy(src, dst, state_sems.at[i])
+        for i, (src, dst) in enumerate(
+            ((sq_rs_hbm, sq_rs), (sq_cs_hbm, sq_cs), (na_rs_hbm, na_rs), (na_cs_hbm, na_cs))
+        )
+    ]
+    for copy in copies[:AHEAD] + states:
         copy.start()
 
     barrier = pltpu.get_barrier_semaphore()
@@ -217,6 +223,9 @@
     @pl.loop(1, wide)
     def _(d):
         rs_copy(d).start()
+
+    for copy in states:
+        copy.wait()
 
     def ag_copy(d):
         peer = lax.rem(me_w + d, wide)
@@ -363,32 +372,72 @@
 
 
 def update_kernel(
-    count,
     sq_g, na_g, sq_rf, sq_cf, na_rf, na_cf, scale,
     sq_out, na_out, sq_rf_out, sq_cf_out, na_rf_out, na_cf_out,
+    sq_slots, na_slots, sq_sems, na_sems, small_sems,
 ):
-    m, q = pl.program_id(0), pl.program_id(1)
-    at = pl.multiple_of(q * LANES, LANES)
-
-    @pl.when((m == 0) & (q == 0))
-    def _():
-        sq_rf_out[...] = sq_rf[...]
-        sq_cf_out[...] = sq_cf[...]
-        na_rf_out[...] = na_rf[...]
-        na_cf_out[...] = na_cf[...]
-
-    for g, rf, cf, out, first in (
-        (sq_g, sq_rf, sq_cf, sq_out, 0),
-        (na_g, na_rf, na_cf, na_out, count),
-    ):
-        rowmul = lax.rsqrt(picked_row(rf[:, pl.ds(at, LANES)], m)) * scale[pl.ds(first + m, 1), :]
-        rowmul = jnp.broadcast_to(rowmul, (LANES, LANES)).T
-        cols = g.shape[2]
-        block = min(cols, 512)
-        for start in range(0, cols, block):
-            colmul = lax.rsqrt(cf[pl.ds(m, 1), pl.ds(start, block)])
-            values = g[0, :, pl.ds(start, block)].astype(jnp.float32)
-            out[0, :, pl.ds(start, block)] = values * tiled(rowmul, block // LANES) * colmul
+    count, rows, sq_cols = sq_g.shape
+    slots = sq_slots.shape[0]
+    per = rows // LANES
+    half = LANES // 2
+    small = [
+        pltpu.make_async_copy(src, dst, small_sems.at[i])
+        for i, (src, dst) in enumerate(
+            ((sq_rf, sq_rf_out), (sq_cf, sq_cf_out), (na_rf, na_rf_out), (na_cf, na_cf_out))
+        )
+    ]
+    for copy in small:
+        copy.start()
+    kinds = (
+        (sq_g, sq_rf, sq_cf, sq_out, sq_slots, sq_sems, 0),
+        (na_g, na_rf, na_cf, na_out, na_slots, na_sems, count),
+    )
+
+    def out_copy(kind, t, h):
+        _, _, _, out, held, sems, _ = kind
+        slot = lax.rem(t, slots)
+        row = pl.multiple_of(lax.rem(t, per) * LANES + h * half, half)
+        return pltpu.make_async_copy(
+            held.at[slot, pl.ds(h * half, half), :],
+            out.at[lax.div(t, per), pl.ds(row, half), :],
+            sems.at[slot, h],
+        )
+
+    def wait(t):
+        for kind in kinds:
+            for h in range(2):
+                out_copy(kind, t, h).wait()
+
+    @pl.loop(0, count * per)
+    def _(t):
+        m, q, slot = lax.div(t, per), lax.rem(t, per), lax.rem(t, slots)
+        at = pl.multiple_of(q * LANES, LANES)
+
+        @pl.when(t >= slots)
+        def _():
+            wait(t - slots)
+
+        for kind in kinds:
+            g, rf, cf, _, held, _, first = kind
+            rowmul = lax.rsqrt(picked_row(rf[:, pl.ds(at, LANES)], m)) * scale[pl.ds(first + m, 1), :]
+            rowmul = jnp.broadcast_to(rowmul, (LANES, LANES)).T
+            cols = g.shape[2]
+            block = min(cols, 512)
+            for h in range(2):
+                rows_at = pl.ds(pl.multiple_of(at + h * half, half), half)
+                mul = rowmul[h * half : (h + 1) * half]
+                for start in range(0, cols, block):
+                    colmul = lax.rsqrt(cf[pl.ds(m, 1), pl.ds(start, block)])
+                    values = g[m, rows_at, pl.ds(start, block)].astype(jnp.float32)
+                    held[slot, pl.ds(h * half, half), pl.ds(start, block)] = (
+                        values * tiled(mul, block // LANES) * colmul
+                    )
+                out_copy(kind, t, h).start()
+
+    for t in range(max(count * per - slots, 0), count * per):
+        wait(t)
+    for copy in small:
+        copy.wait()
 
 
 def kernel_per_device(wide, narrow, square_grads, narrow_grads, *states):
@@ -396,25 +445,33 @@
     na_cols = narrow_grads.shape[2]
     f32 = jnp.float32
     vmem = pl.BlockSpec(memory_space=pltpu.VMEM)
-    hbm = pl.BlockSpec(memory_space=pl.ANY)
+    hbm = pl.BlockSpec(memory_space=pltpu.HBM)
     shape = jax.ShapeDtypeStruct
     table_rows = count * (sq_cols + na_cols) // LANES // wide
     chunks = count * (sq_cols // column_block(sq_cols) + na_cols // column_block(na_cols))
     dma = pltpu.SemaphoreType.DMA
+    slots = 3
     factors = (
         shape((count, rows), f32),
         shape((count, sq_cols), f32),
         shape((count, rows), f32),
         shape((count, na_cols), f32),
     )
-    stats = pl.pallas_call(
+    *stats, square_held, narrow_held = pl.pallas_call(
         functools.partial(stats_kernel, wide, narrow),
-        out_shape=factors + (shape((2 * count, LANES), f32),),
-        in_specs=[hbm, hbm, vmem, vmem, vmem, vmem],
-        out_specs=[vmem] * 5,
+        out_shape=factors
+        + (
+            shape((2 * count, LANES), f32),
+            shape(square_grads.shape, square_grads.dtype),
+            shape(narrow_grads.shape, narrow_grads.dtype),
+        ),
+        in_specs=[hbm] * 6,
+        out_specs=[vmem] * 7,
         scratch_shapes=[
-            pltpu.VMEM((count, rows, sq_cols), square_grads.dtype),
-            pltpu.VMEM((count, rows, na_cols), narrow_grads.dtype),
+            pltpu.VMEM((count, rows), f32),
+            pltpu.VMEM((count, sq_cols), f32),
+            pltpu.VMEM((count, rows), f32),
+            pltpu.VMEM((count, na_cols), f32),
             pltpu.VMEM((rows, LANES), f32),
             pltpu.VMEM((rows, LANES), f32),
             pltpu.VMEM((2 * count, rows // LANES, LANES), f32),
@@ -427,6 +484,7 @@
             pltpu.VMEM((4 * count, LANES), f32),
             pltpu.VMEM((wide * narrow, 1, LANES), f32),
             dma((chunks,)),
+            dma((4,)),
             dma((2 * count,)),
             dma((2 * count,)),
             dma((wide,)),
@@ -437,31 +495,30 @@
             dma((wide * narrow,)),
         ],
         compiler_params=pltpu.CompilerParams(
-            collective_id=0, has_side_effects=True, vmem_limit_bytes=40 * 2**20
+            collective_id=0, has_side_effects=True, vmem_limit_bytes=12 * 2**20
         ),
         name="stats",
-    )(square_grads, narrow_grads, *states)
-
-    full = lambda s: pl.BlockSpec(s.shape, lambda m, q: (0, 0))
-    blocked = lambda cols: pl.BlockSpec((1, LANES, cols), lambda m, q: (m, q, 0))
-    square_update, narrow_update, *small = pl.pallas_call(
-        functools.partial(update_kernel, count),
-        grid=(count, rows // LANES),
+    )(*(pltpu.with_memory_space_constraint(x, pltpu.HBM) for x in (square_grads, narrow_grads, *states)))
+
+    return pl.pallas_call(
+        update_kernel,
         out_shape=(
             shape(square_grads.shape, f32),
             shape(narrow_grads.shape, f32),
         )
         + factors,
-        in_specs=[blocked(sq_cols), blocked(na_cols)]
-        + [full(s) for s in factors]
-        + [pl.BlockSpec((2 * count, LANES), lambda m, q: (0, 0))],
-        out_specs=[blocked(sq_cols), blocked(na_cols)] + [full(s) for s in factors],
-        compiler_params=pltpu.CompilerParams(
-            dimension_semantics=("arbitrary", "arbitrary"), vmem_limit_bytes=20 * 2**20
-        ),
+        in_specs=[vmem] * 7,
+        out_specs=[hbm] * 6,
+        scratch_shapes=[
+            pltpu.VMEM((slots, LANES, sq_cols), f32),
+            pltpu.VMEM((slots, LANES, na_cols), f32),
+            dma((slots, 2)),
+            dma((slots, 2)),
+            dma((4,)),
+        ],
+        compiler_params=pltpu.CompilerParams(vmem_limit_bytes=12 * 2**20),
         name="update",
-    )(square_grads, narrow_grads, *stats)
-    return (square_update, narrow_update, *small)
+    )(square_held, narrow_held, *stats)
 
 
 def solution(mesh):

time: 52.3 us -> 43.8 us (0.84)
  local copies, waits for them, and re-layouts: 5.8 us -> 0 us
  Pallas kernels: 45.5 us -> 43 us
    unnamed x12 -> x0, local copies, waits for them, and re-layouts: 5.8 us -> none
    pallas_call x1, Pallas kernels: 15 us -> 12.5 us  [kernel_per_device(): pl.pallas_call(update_kernel, out_shape=(shape(square_grads.shape, f32),...]
where the time goes in v2:
time: 43.8 us; the launch traced here: 43.7 us
  Pallas kernels  43 us (98%)
  between operations  0.64 us (1%)
    pallas_call x1, Pallas kernels, kernel_per_device(): pl.pallas_call(functools.partial(stats_kernel, wide, narrow), out_shape=f...  30.5 us
    pallas_call x1, Pallas kernels, kernel_per_device(): pl.pallas_call(update_kernel, out_shape=(shape(square_grads.shape, f32),...  12.5 us

profile of v2, /device:TPU:0, one launch (start us, length us, event | category | flops | bytes accessed | tf_op | source)
XLA Modules:
  0.0 43.7 jit_solution(9251302726371879073)
XLA Ops:
  0.6 30.5 %stats.1 = (f32[4,512]{1,0:T(4,128)S(1)}, f32[4,4096]{1,0:T(4,128)S(1)}, f32[4,512]{1,0:T(4,128)S(1)}, f32[4,512]{1,0:T(4,128)S(1)}, f32[8,128]{1,0:T(8,128)S(1)...) custom-call(bf16[4,512,4096]{2,1,0:T(8,128)(2,1)} %sq_hbm.1, bf16[4,512,512]{2,1,0:T(8,128)(2,1)} %na_hbm.1, ...), custom_call_target="tpu_custom_call" | custom-call | tf_op jit(solution)/shard_map/stats/pallas_call | solution.py:460
  31.2 12.5 %update.1 = (f32[4,512,4096]{2,1,0:T(8,128)}, f32[4,512,512]{2,1,0:T(8,128)}, f32[4,512]{1,0:T(4,128)}, f32[4,4096]{1,0:T(4,128)}, f32[4,512]{1,0:T(4,128)}, /*index=5*/f32[4,512]{1,0:T(4,128)}) custom-call(bf16[4,512,4096]{2,1,0:T(8,128)(2,1)S(1)} %get-tuple-element.13.sq_g, bf16[4,512,512]{2,1,0:T(8,128)(2,1)S(1)} %get-tuple-element.14.na_g, ...), custom_call_target="tpu_custom_call" | custom-call | tf_op jit(solution)/shard_map/update/pallas_call | solution.py:503

commit v3 on v2

--- a/solution.py
+++ b/solution.py
@@ -11,7 +11,7 @@
 epsilon_square = 1e-30
 clip_limit = 1.0
 LANES = 128
-AHEAD = 6
+AHEAD = 8
 
 
 def square_sums(grads):
@@ -196,7 +196,7 @@
                 return acc + fold(squares)
 
             acc = lax.fori_loop(
-                0, rows // step, body, jnp.zeros((8, block), jnp.float32), unroll=2
+                0, rows // step, body, jnp.zeros((8, block), jnp.float32), unroll=4
             )
             sums = jnp.sum(acc, axis=0, keepdims=True)
             for b in range(block // LANES):
@@ -291,7 +291,7 @@
                 return acc + fold(values * values * inv)
 
             w[m, :, start : start + block] = lax.fori_loop(
-                0, rows // step, body, jnp.zeros((8, block), jnp.float32), unroll=2
+                0, rows // step, body, jnp.zeros((8, block), jnp.float32), unroll=4
             )
 
     @pl.loop(1, wide)

time: 43.8 us -> 42.5 us (0.970)
  Pallas kernels: 43 us -> 41.7 us
    pallas_call x1, Pallas kernels: 30.5 us -> 29.2 us  [kernel_per_device(): pl.pallas_call(functools.partial(stats_kernel, wide, narrow), out_shape=f...]
where the time goes in v3:
time: 42.5 us; the launch traced here: 42.3 us
  Pallas kernels  41.7 us (98%)
  between operations  0.64 us (2%)
    pallas_call x1, Pallas kernels, kernel_per_device(): pl.pallas_call(functools.partial(stats_kernel, wide, narrow), out_shape=f...  29.2 us
    pallas_call x1, Pallas kernels, kernel_per_device(): pl.pallas_call(update_kernel, out_shape=(shape(square_grads.shape, f32),...  12.5 us

profile of v3, /device:TPU:0, one launch (start us, length us, event | category | flops | bytes accessed | tf_op | source)
XLA Modules:
  0.0 42.3 jit_solution(9522965629167123371)
XLA Ops:
  0.6 29.2 %stats.1 = (f32[4,512]{1,0:T(4,128)S(1)}, f32[4,4096]{1,0:T(4,128)S(1)}, f32[4,512]{1,0:T(4,128)S(1)}, f32[4,512]{1,0:T(4,128)S(1)}, f32[8,128]{1,0:T(8,128)S(1)...) custom-call(bf16[4,512,4096]{2,1,0:T(8,128)(2,1)} %sq_hbm.1, bf16[4,512,512]{2,1,0:T(8,128)(2,1)} %na_hbm.1, ...), custom_call_target="tpu_custom_call" | custom-call | tf_op jit(solution)/shard_map/stats/pallas_call | solution.py:460
  29.8 12.5 %update.1 = (f32[4,512,4096]{2,1,0:T(8,128)}, f32[4,512,512]{2,1,0:T(8,128)}, f32[4,512]{1,0:T(4,128)}, f32[4,4096]{1,0:T(4,128)}, f32[4,512]{1,0:T(4,128)}, /*index=5*/f32[4,512]{1,0:T(4,128)}) custom-call(bf16[4,512,4096]{2,1,0:T(8,128)(2,1)S(1)} %get-tuple-element.13.sq_g, bf16[4,512,512]{2,1,0:T(8,128)(2,1)S(1)} %get-tuple-element.14.na_g, ...), custom_call_target="tpu_custom_call" | custom-call | tf_op jit(solution)/shard_map/update/pallas_call | solution.py:503
